TPU v7x, 32 devices: a whole 2x2x4 slice. The times are simulated.
32 devices in a mesh: task: 4 (over z), mp: 8 (over y, x, core).
Axes of the slice: x: 2, y: 2, z: 4, core: 2. Of those that a mesh axis runs over, the one named last changes fastest.
Arguments:
- deter: float32 [1024, 4096], P('task', 'mp'), may hold values from -3 to 3
- draws: int32 [4, 32, 1024], P(None, None, 'task'), may hold values from 0 to 31
- actions: int32 [4, 1024], P(None, 'task'), may hold values from 0 to 17
- horizons: int32 [64], replicated, may hold values from 5 to 30, as said below
- offsets: int32 [4, 4], replicated, may hold values from 0 to 3, as said below
- embed_stoch: bfloat16 [1024, 1024], replicated, may hold values from -1 to 1
- embed_act: bfloat16 [18, 1024], replicated, may hold values from -6 to 6
- gru_weight: bfloat16 [5120, 3, 4096], P(None, None, 'mp'), may hold values from -0.078125 to 0.078125
- prior_weight: bfloat16 [4096, 1024], replicated, may hold values from -0.09375 to 0.09375
- logit_weight: bfloat16 [1024, 1024], replicated, may hold values from -0.75 to 0.75
- head_weight: bfloat16 [1024, 2], replicated, may hold values from -0.375 to 0.375
Outputs:
- log_prob: float32 [4, 1024], P(None, 'task')
- reward: float32 [4, 1024], P(None, 'task')
- continuation: float32 [4, 1024], P(None, 'task')
- final_deter: float32 [1024, 4096], P('task', 'mp')
Inputs may be any that keep to these rules, and one draw needn't show every extreme that they name: `horizons`: rows of task k are home rows k * (16) up to (k + 1) * 16 - 1. `offsets`: the 4 numbers of one row are distinct.
All inputs are finite; a program needn't handle non-finite values.
Results may differ from a plain program's by a relative error of at most 0.0045.
Values may be sent and summed in bfloat16 or wider, within the bound.
A program may use at most 128 MiB of HBM per device.

v0:
```python
import functools

import jax
import jax.numpy as jnp
from jax import lax
from jax.experimental import pallas as pl
from jax.experimental.pallas import tpu as pltpu
from jax.sharding import PartitionSpec as P

HID = 1024
GROUPS = 32
CLASSES = 32
ACTS = 18
TASKS = 64
BLK_DEV = 4
STEPS = 4
WSTART = 16


def normed_rows(values):
    entries = values.shape[-1]
    average = jnp.sum(values, axis=-1, keepdims=True) / entries
    squares = jnp.sum(values * values, axis=-1, keepdims=True) / entries
    return (values - average) * lax.rsqrt(squares - average * average + 1e-05)


def product(rows_in, weight):
    return jnp.dot(rows_in, weight, preferred_element_type=jnp.float32)


def flipped(index, mask):
    bit = 1
    while bit <= mask:
        if mask & bit:
            index = index + bit * (1 - 2 * ((index // bit) % 2))
        bit *= 2
    return index


def window_kernel(
    shards,
    groups,
    rows,
    share,
    deter_ref,
    embedded_ref,
    living_ref,
    weight_ref,
    carried_ref,
    lows_ref,
    weight,
    gath,
    parts,
    stats,
    weight_sem,
    low_sem,
    send_sem,
    recv_sem,
    stat_send,
    stat_recv,
):
    me = lax.axis_index("mp")
    peers = {mask: flipped(me, mask) for mask in range(1, shards)}
    fetch = pltpu.make_async_copy(weight_ref, weight, weight_sem)
    fetch.start()
    barrier = pltpu.get_barrier_semaphore()
    for mask in range(1, shards):
        pl.semaphore_signal(
            barrier,
            inc=1,
            device_id={"mp": peers[mask]},
            device_id_type=pl.DeviceIdType.MESH,
        )
    bits = []
    bit = shards // 2
    while bit:
        bits.append(bit)
        bit //= 2
    orders = [bits, [bits[1], bits[0]] + bits[2:]]
    half = rows // 2
    masks = sorted(range(1, shards), key=lambda mask: (mask.bit_count(), mask))

    def source(mask):
        return me if mask == 0 else peers[mask]

    def hop(g, s, mask, via):
        block = gath.at[g, source(mask), pl.ds(s * half, half)]
        return pltpu.make_async_remote_copy(
            src_ref=block,
            dst_ref=block,
            send_sem=send_sem.at[g, s, mask ^ via],
            recv_sem=recv_sem.at[g, s, mask ^ via],
            device_id={"mp": peers[via]},
            device_id_type=pl.DeviceIdType.MESH,
        )

    def forward(g, s, mask):
        order = orders[s]
        last = max([order.index(bit) for bit in order if mask & bit], default=-1)
        for via in order[last + 1 :]:
            hop(g, s, mask, via).start()

    def arriving(g, s, mask):
        block = gath.at[g, source(mask), pl.ds(s * half, half)]
        return pltpu.make_async_remote_copy(
            src_ref=block,
            dst_ref=block,
            send_sem=send_sem.at[g, s, mask],
            recv_sem=recv_sem.at[g, s, mask],
            device_id={"mp": peers[mask]},
            device_id_type=pl.DeviceIdType.MESH,
        )

    def launch(g):
        here = pl.ds(g * rows, rows)
        gath[g, me] = carried_ref[here, :].astype(jnp.bfloat16)
        for s in range(2):
            forward(g, s, 0)

    def stat_copy(g, mask):
        return pltpu.make_async_remote_copy(
            src_ref=stats.at[g, 0],
            dst_ref=stats.at[g, mask],
            send_sem=stat_send.at[g, mask],
            recv_sem=stat_recv.at[g, mask],
            device_id={"mp": peers[mask]},
            device_id_type=pl.DeviceIdType.MESH,
        )

    def multiply(g, rows_in, start, depth, first):
        for part in range(3):
            term = jnp.dot(
                rows_in, weight[part, pl.ds(start, depth), :], preferred_element_type=jnp.float32
            )
            if first:
                parts[g, part] = term
            else:
                parts[g, part] += term

    carried_ref[...] = deter_ref[...]
    pl.semaphore_wait(barrier, shards - 1)
    for g in range(groups):
        launch(g)
    fetch.wait()

    def step(t, _):
        for g in range(groups):
            seen = set()

            def need(s, mask):
                if (s, mask) not in seen:
                    seen.add((s, mask))
                    arriving(g, s, mask).wait_recv()
                    forward(g, s, mask)

            multiply(g, embedded_ref[t, pl.ds(g * rows, rows), :], 0, HID, True)
            for s in range(2):
                need(s, orders[s][0])
            for mask in [0] + masks:
                if mask:
                    for s in range(2):
                        need(s, mask)
                start = pl.multiple_of(HID + source(mask) * share, share)
                multiply(g, gath[g, source(mask)], start, share, False)
            keep = pltpu.make_async_copy(gath.at[g], lows_ref.at[t, g], low_sem)
            keep.start()
            sums = jnp.zeros((rows, 128), jnp.float32)
            squares = jnp.zeros((rows, 128), jnp.float32)
            for part in range(3):
                for column in range(0, share, 128):
                    piece = parts[g, part, :, pl.ds(column, 128)]
                    sums = sums + piece
                    squares = squares + piece * piece
            stats[g, 0, 0:1, :] = jnp.sum(sums.T, axis=0, keepdims=True)
            stats[g, 0, 1:2, :] = jnp.sum(squares.T, axis=0, keepdims=True)
            for s in range(2):
                for mask in masks:
                    arriving(g, s, mask).wait_send()
            keep.wait()
            for mask in masks:
                stat_copy(g, mask).start()
        for g in range(groups):
            for mask in masks:
                stat_copy(g, mask).wait()
            total = jnp.sum(stats[g], axis=0) / (3 * share * shards)
            average = jnp.broadcast_to(total[0:1], (128, rows)).T
            square = jnp.broadcast_to(total[1:2], (128, rows)).T
            inverse = lax.rsqrt(square - average * average + 1e-05)
            here = pl.ds(g * rows, rows)
            alive = living_ref[t, here, :]
            for column in range(0, share, 128):
                where = pl.ds(column, 128)
                normed = [(parts[g, part, :, where] - average) * inverse for part in range(3)]
                reset_gate = jax.nn.sigmoid(normed[0])
                candidate = jnp.tanh(reset_gate * normed[1])
                update = jax.nn.sigmoid(normed[2] - 1.0)
                before = carried_ref[here, where]
                renewed = update * candidate + (1.0 - update) * before
                carried_ref[here, where] = jnp.where(alive > 0, renewed, before)

            @pl.when(t < STEPS - 1)
            def _():
                launch(g)

        return 0

    lax.fori_loop(0, STEPS, step, 0)


def recurrence(deter, embedded, gate_weight, living, shards):
    rows_here, share = deter.shape
    groups = 2
    rows = rows_here // groups
    alive = jnp.broadcast_to(living[:, :, None], (STEPS, rows_here, 128))
    vmem = pl.BlockSpec(memory_space=pltpu.VMEM)
    hbm = pl.BlockSpec(memory_space=pl.ANY)
    dma = pltpu.SemaphoreType.DMA
    return pl.pallas_call(
        functools.partial(window_kernel, shards, groups, rows, share),
        out_shape=(
            jax.ShapeDtypeStruct((rows_here, share), jnp.float32),
            jax.ShapeDtypeStruct((STEPS, groups, shards, rows, share), jnp.bfloat16),
        ),
        in_specs=[vmem, vmem, vmem, hbm],
        out_specs=(vmem, hbm),
        scratch_shapes=[
            pltpu.VMEM(gate_weight.shape, jnp.bfloat16),
            pltpu.VMEM((groups, shards, rows, share), jnp.bfloat16),
            pltpu.VMEM((groups, 3, rows, share), jnp.float32),
            pltpu.VMEM((groups, shards, 2, rows), jnp.float32),
            dma,
            dma,
            dma((groups, 2, shards)),
            dma((groups, 2, shards)),
            dma((groups, shards)),
            dma((groups, shards)),
        ],
        compiler_params=pltpu.CompilerParams(
            collective_id=0, has_side_effects=True, vmem_limit_bytes=48 * 1024 * 1024
        ),
    )(deter, embedded, alive, gate_weight)


def spread_kernel(axis, count, block_ref, out_ref, send_sem, recv_sem):
    me = lax.axis_index(axis)
    barrier = pltpu.get_barrier_semaphore()
    for ahead in range(1, count):
        pl.semaphore_signal(
            barrier,
            inc=1,
            device_id={axis: (me + ahead) % count},
            device_id_type=pl.DeviceIdType.MESH,
        )
    pl.semaphore_wait(barrier, count - 1)

    def copy(ahead, slot):
        return pltpu.make_async_remote_copy(
            src_ref=block_ref,
            dst_ref=out_ref.at[slot],
            send_sem=send_sem.at[ahead],
            recv_sem=recv_sem.at[ahead],
            device_id={axis: (me + ahead) % count},
            device_id_type=pl.DeviceIdType.MESH,
        )

    for ahead in range(1, count):
        copy(ahead, me).start()
    out_ref[me] = block_ref[...]
    for ahead in range(1, count):
        copy(ahead, me).wait_send()
        copy(ahead, (me + count - ahead) % count).wait_recv()


def spread(block, axis, collective_id):
    count = lax.axis_size(axis)
    vmem = pl.BlockSpec(memory_space=pltpu.VMEM)
    return pl.pallas_call(
        functools.partial(spread_kernel, axis, count),
        out_shape=jax.ShapeDtypeStruct((count,) + block.shape, block.dtype),
        in_specs=[vmem],
        out_specs=vmem,
        scratch_shapes=[
            pltpu.SemaphoreType.DMA((count,)),
            pltpu.SemaphoreType.DMA((count,)),
        ],
        compiler_params=pltpu.CompilerParams(
            collective_id=collective_id, has_side_effects=True
        ),
    )(block)


def on_device(
    deter,
    draws,
    actions,
    horizons,
    offsets,
    embed_stoch,
    embed_act,
    gru_weight,
    prior_weight,
    logit_weight,
    head_weight,
):
    holders = lax.axis_size("task")
    device = lax.axis_index("task")
    shards = lax.axis_size("mp")
    shard_index = lax.axis_index("mp")
    rows_here, det_share = deter.shape
    block_rows = rows_here // BLK_DEV
    per_task = rows_here * holders // TASKS
    own_rows = rows_here // shards
    places = jnp.arange(holders, dtype=jnp.int32)
    classes = jnp.arange(CLASSES, dtype=jnp.int32)
    running = jnp.cumsum(offsets, axis=0) % holders
    packed = jnp.concatenate([draws, actions[:, None]], axis=1).astype(jnp.bfloat16)
    packed = spread(packed, "task", 1)
    packed = packed.reshape(holders, STEPS, GROUPS + 1, BLK_DEV, block_rows)
    at_slot = (device + running) % holders
    picked = places[:, None, None] == at_slot[None]
    packed = jnp.sum(
        jnp.where(picked[:, :, None, :, None], packed.astype(jnp.float32), 0.0), axis=0
    ).astype(jnp.int32)
    packed = packed.reshape(STEPS, GROUPS + 1, rows_here)
    draws_home = jnp.transpose(packed[:, :GROUPS], (0, 2, 1))
    hot = (draws_home[:, :, :, None] == classes).astype(jnp.bfloat16)
    hot = hot.reshape(STEPS * rows_here, GROUPS * CLASSES)
    action_hot = (
        packed[:, GROUPS].reshape(-1)[:, None] == jnp.arange(ACTS, dtype=jnp.int32)
    ).astype(jnp.bfloat16)
    embed_pre = product(hot, embed_stoch) + product(action_hot, embed_act)
    embedded = jax.nn.silu(normed_rows(embed_pre)).astype(jnp.bfloat16)
    embedded = embedded.reshape(STEPS, rows_here, HID)

    home_rows = device * rows_here + jnp.arange(rows_here, dtype=jnp.int32)
    task_ids = jnp.arange(TASKS, dtype=jnp.int32)
    horizon_rows = jnp.sum(
        jnp.where((home_rows // per_task)[:, None] == task_ids, horizons, 0), axis=1
    )
    alive = horizon_rows[None] > WSTART + jnp.arange(STEPS, dtype=jnp.int32)[:, None]
    living = alive.astype(jnp.float32)

    gate_weight = jnp.transpose(gru_weight, (1, 0, 2))
    carried, lows = recurrence(deter, embedded, gate_weight, living, shards)

    target = (device + running[-1]) % holders
    sending = places[:, None] == target[None, :]
    blocks = carried.reshape(BLK_DEV, block_rows, det_share)
    outgoing = jnp.where(sending[:, :, None, None], blocks[None], 0.0).astype(jnp.bfloat16)
    arrived = lax.all_to_all(
        outgoing.reshape(holders * BLK_DEV * block_rows, det_share),
        "task",
        split_axis=0,
        concat_axis=0,
        tiled=True,
    ).reshape(holders, BLK_DEV, block_rows, det_share)
    taking = places[:, None] == ((device - running[-1]) % holders)[None, :]
    final = jnp.sum(
        jnp.where(taking[:, :, None, None], arrived.astype(jnp.float32), 0.0), axis=0
    ).reshape(rows_here, det_share)

    def own(array, axis):
        return lax.dynamic_slice_in_dim(array, shard_index * own_rows, own_rows, axis)

    first = shard_index * own_rows
    group_rows = lows.shape[3]
    state_rows = lax.dynamic_slice(
        lows,
        (0, first // group_rows, 0, first % group_rows, 0),
        (STEPS, 1, shards, own_rows, det_share),
    )
    state_rows = jnp.transpose(state_rows, (0, 1, 3, 2, 4)).reshape(STEPS * own_rows, -1)
    hidden = jax.nn.silu(normed_rows(product(state_rows, prior_weight))).astype(jnp.bfloat16)
    raw = product(hidden, logit_weight).reshape(STEPS * own_rows, GROUPS, CLASSES)
    exponent = jnp.exp(5.0 * jnp.tanh(raw / 5.0))
    own_hot = own(draws_home, 1).reshape(STEPS * own_rows, GROUPS)[:, :, None] == classes
    chosen = jnp.sum(jnp.where(own_hot, exponent, 0.0), axis=-1)
    chances = 0.99 * chosen / jnp.sum(exponent, axis=-1) + 0.01 / CLASSES
    log_prob = jnp.sum(jnp.log(chances), axis=-1)
    head_out = product(hidden, head_weight)
    results = jnp.stack([log_prob, head_out[:, 0], jax.nn.sigmoid(head_out[:, 1])])
    results = results.reshape(3, STEPS, own_rows) * own(living, 1)[None]
    results = spread(results.reshape(3 * STEPS, own_rows), "mp", 2)
    results = spread(results, "task", 3)
    results = results.reshape(holders, shards, 3, STEPS, own_rows)
    results = jnp.transpose(results, (0, 2, 3, 1, 4)).reshape(
        holders, 3, STEPS, BLK_DEV, block_rows
    )
    source = (device - running) % holders
    from_home = places[:, None, None] == source[None]
    outs = jnp.sum(jnp.where(from_home[:, None, :, :, None], results, 0.0), axis=0)
    outs = outs.reshape(3, STEPS, rows_here)
    return (outs[0], outs[1], outs[2], final)


def solution(mesh):
    in_specs = (
        P("task", "mp"),
        P(None, None, "task"),
        P(None, "task"),
        P(),
        P(),
        P(),
        P(),
        P(None, None, "mp"),
        P(),
        P(),
        P(),
    )
    out_specs = (P(None, "task"), P(None, "task"), P(None, "task"), P("task", "mp"))
    return jax.shard_map(
        on_device, mesh=mesh, in_specs=in_specs, out_specs=out_specs, check_vma=False
    )
```

profile of v0, /device:TPU:0, one launch (start us, length us, event | category | flops | bytes accessed | tf_op | source)
XLA Modules:
  0.0 142.9 jit_solution(2244708031004843212)
XLA Ops:
  0.6 0.0 copy-start
  0.7 0.9 reduce_window_sum.11
  1.6 0.7 convert_bitcast_fusion
  2.3 0.1 broadcast_in_dim.120
  2.4 0.1 broadcast_in_dim.121
  2.5 0.9 convert.7
  3.4 0.6 pad_maximum_fusion.block_ref
  4.0 13.0 %shard_map.138 = bf16[4,4,33,256]{3,2,1,0:T(8,128)(2,1)} custom-call(bf16[4,33,256]{2,1,0:T(8,128)(2,1)} %pad_maximum_fusion.block_ref), custom_call_target="tpu_custom_call" | custom-call | tf_op jit(solution)/shard_map/pallas_call | solution.py:277
  17.0 1.1 select_reduce_fusion.1
  18.2 0.1 broadcast_in_dim.133
  18.2 0.1 broadcast_in_dim.134
  18.3 0.1 eq.157
  18.4 0.1 copy.42
  18.5 0.5 eq.154
  19.1 0.0 copy-start.5
  19.1 1.0 copy.46
  20.1 0.0 copy-done.5
  20.1 0.1 select_reduce_fusion.4
  20.2 0.1 compare_convert_fusion
  20.3 0.0 copy-done
  20.3 0.0 copy-start.3
  20.3 2.5 %fusion = f32[1024,1024]{1,0:T(8,128)S(1)} fusion(bf16[1024,1024]{1,0:T(8,128)(2,1)S(1)} %copy-done, s32[1024,1024]{0,1:T(8,128)S(1)} %bitcast.51, s32[1024]{0:T(1024)S(1)} %eq.157), kind=kOutput, calls=%fused_computation.2 | convolution fusion | flops 2148532224 | bytes 10489856 | tf_op jit(solution)/shard_map/dot_general | solution.py:28
  22.7 0.0 copy-done.3
  22.7 1.1 fusion.14
  23.8 0.0 copy-start.2
  23.8 1.6 %multiply_convert_fusion = bf16[1024,1024]{1,0:T(8,128)(2,1)S(1)} fusion(f32[1024,1024]{1,0:T(8,128)S(1)} %get-tuple-element.29, f32[1024]{0:T(1024)S(1)} %get-tuple-element.24, f32[1024]{0:T(1024)S(1)} %get-tuple-element.23), kind=kLoop, calls=%fused_computation | loop fusion | flops 7340032 | bytes 6299648 | tf_op jit(solution)/shard_map/convert_element_type | solution.py:332
  25.4 0.2 broadcast_in_dim.127.living_ref
  25.6 0.0 copy-done.2
  25.7 75.0 %shard_map.139 = (f32[256,512]{1,0:T(8,128)S(1)}, bf16[4,2,8,128,512]{4,3,2,1,0:T(8,128)(2,1)}) custom-call(f32[256,512]{1,0:T(8,128)S(1)} %copy-done.2, bf16[4,256,1024]{2,1,0:T(8,128)(2,1)S(1)} %bitcast.47, f32[4,256,128]{2,1,0:T(8,128)S(1)} %broadcast_in_dim.127.living_ref, bf16[3,5120,512]{2,1,0:T(8,128)(2,1)} %bitcast.49), custom_call_target="tpu_custom_call" | custom-call | tf_op jit(solution)/shard_map/pallas_call | solution.py:218
  100.7 1.3 select_convert_fusion
  101.9 5.4 %all-to-all-start = ((bf16[4,256,512]{2,1,0:T(8,128)(2,1)}), bf16[4,256,512]{2,1,0:T(8,128)(2,1)S(1)}, u32[]{:S(2)}, u32[]{:S(2)}) async-start(bf16[4,256,512]{2,1,0:T(8,128)(2,1)} %select_convert_fusion), calls=%async_computation | async-start | bytes 2097152 | tf_op jit(solution)/shard_map/all_to_all | solution.py:350
  107.4 0.1 copy.38
  107.5 0.1 broadcast_in_dim.130
  107.6 0.1 broadcast_in_dim.131
  107.6 0.1 copy.39
  107.8 0.1 dynamic-slice_bitcast_fusion.1
  107.9 0.1 eq.150
  108.0 1.3 dynamic-slice_bitcast_fusion
  109.4 0.6 copy.43
  110.0 0.4 copy.47
  110.4 0.0 copy-start.4
  110.4 4.7 %fusion.15 = (f32[128]{0:T(128)S(1)}, f32[128]{0:T(128)S(1)}, f32[128,1024]{1,0:T(8,128)S(1)}) fusion(bf16[128,4096]{1,0:T(8,128)(2,1)S(1)} %bitcast.50, bf16[4096,1024]{1,0:T(8,128)(2,1)} %param.19), kind=kOutput, calls=%fused_computation.70 | convolution fusion | flops 1074134784 | bytes 9962496 | tf_op jit(solution)/shard_map/dot_general | solution.py:28
  115.1 0.0 copy-start.1
  115.1 0.3 multiply_convert_fusion.1
  115.4 0.0 copy-done.4
  115.4 0.2 fusion.18
  115.6 0.1 stack.10
  115.7 0.1 div.76
  115.8 2.9 %fusion.5 = f32[128,1024]{1,0:T(8,128)} fusion(bf16[128,1024]{1,0:T(8,128)(2,1)S(1)} %multiply_convert_fusion.1, bf16[1024,1024]{1,0:T(8,128)(2,1)} %param.20), kind=kOutput, calls=%fused_computation.11 | convolution fusion | flops 268697600 | bytes 2883584 | tf_op jit(solution)/shard_map/dot_general | solution.py:28
  118.7 2.0 %copy.44 = f32[128,1024]{0,1:T(8,128)} copy(f32[128,1024]{1,0:T(8,128)} %fusion.5) | data formatting | bytes 1048576 | tf_op jit(solution)/shard_map/exp | solution.py:375
  120.7 1.3 select_reduce_fusion.2
  122.0 0.1 stack.9
  122.1 0.1 constant_dynamic-slice_fusion
  122.2 0.6 mul.93.block_ref
  122.8 6.0 %shard_map.140.block_ref = f32[8,12,32]{2,1,0:T(8,128)} custom-call(f32[12,32]{1,0:T(8,128)} %mul.93.block_ref), custom_call_target="tpu_custom_call" | custom-call | tf_op jit(solution)/shard_map/pallas_call | solution.py:277
  128.8 9.9 %shard_map.141 = f32[4,8,12,32]{3,2,1,0:T(8,128)} custom-call(f32[8,12,32]{2,1,0:T(8,128)} %shard_map.140.block_ref), custom_call_target="tpu_custom_call" | custom-call | tf_op jit(solution)/shard_map/pallas_call | solution.py:277
  138.7 1.0 copy.45
  139.7 0.1 select_reduce_fusion.3
  139.8 0.7 squeeze.14
  140.5 0.7 squeeze.13
  141.2 0.7 squeeze.12
  141.8 0.0 all-to-all-done
  141.8 1.1 select_reduce_fusion
  142.9 0.0 copy-done.1
  (21 shorter events, 0.3 us)
Async XLA Ops:
  0.6 19.6 %copy-start = (bf16[1024,1024]{1,0:T(8,128)(2,1)S(1)}, bf16[1024,1024]{1,0:T(8,128)(2,1)}, u32[]{:S(2)}) copy-start(bf16[1024,1024]{1,0:T(8,128)(2,1)} %param.16) | copy-start | bytes 6291460
  19.1 1.0 copy-start.5
  20.3 2.5 %copy-start.3 = (bf16[18,1024]{1,0:T(8,128)(2,1)S(1)}, bf16[18,1024]{1,0:T(8,128)(2,1)}, u32[]{:S(2)}) copy-start(bf16[18,1024]{1,0:T(8,128)(2,1)} %param.17) | copy-start | bytes 110596
  23.8 1.8 %copy-start.2 = (f32[256,512]{1,0:T(8,128)S(1)}, f32[256,512]{1,0:T(8,128)}, u32[]{:S(2)}) copy-start(f32[256,512]{1,0:T(8,128)} %deter_ref.1) | copy-start | bytes 1572868
  101.9 39.9 %all-to-all-start = ((bf16[4,256,512]{2,1,0:T(8,128)(2,1)}), bf16[4,256,512]{2,1,0:T(8,128)(2,1)S(1)}, u32[]{:S(2)}, u32[]{:S(2)}) async-start(bf16[4,256,512]{2,1,0:T(8,128)(2,1)} %select_convert_fusion), calls=%async_computation | async-start | bytes 2097152 | tf_op jit(solution)/shard_map/all_to_all | solution.py:350
  110.4 5.0 %copy-start.4 = (bf16[1024,2]{0,1:T(2,128)(2,1)S(1)}, bf16[1024,2]{0,1:T(2,128)(2,1)}, u32[]{:S(2)}) copy-start(bf16[1024,2]{0,1:T(2,128)(2,1)} %param.21) | copy-start | bytes 12292
  115.1 27.8 %copy-start.1 = (bf16[1024,1024]{1,0:T(8,128)(2,1)S(1)}, bf16[1024,1024]{1,0:T(8,128)(2,1)}, u32[]{:S(2)}) copy-start(bf16[1024,1024]{1,0:T(8,128)(2,1)} %param.16) | copy-start | bytes 6291460
where the time goes:
time: 144 us; the launch traced here: 143 us
  Pallas kernels  104 us (72%)
  matrix products  11.3 us (8%)
  local copies, waits for them, and re-layouts  11.2 us (8%)
  other arithmetic  10.1 us (7%)
  starting transfers between devices  5.44 us (4%)
    pallas_call x1, Pallas kernels, recurrence(): pl.pallas_call(functools.partial(window_kernel, shards, groups, rows, sha...  75 us
    pallas_call x3, Pallas kernels, spread(): pl.pallas_call(functools.partial(spread_kernel, axis, count), out_shape=j...  28.9 us
    dot_general x5, matrix products, product(): return jnp.dot(rows_in, weight, preferred_element_type=jnp.float32)  11.3 us
    all_to_all x1, starting transfers between devices, on_device(): lax.all_to_all(outgoing.reshape(holders * BLK_DEV * block_rows, det_share...  5.44 us
  transfers between devices with their start and end apart: 1, of which 0 were waited for; matrix products, arithmetic and copies ran while one was open for 13% of the time, Pallas kernels for 11%

commit v1 on v0

v1 whole, which is shorter than its diff:
```python
import functools

import jax
import jax.numpy as jnp
from jax import lax
from jax.experimental import pallas as pl
from jax.experimental.pallas import tpu as pltpu
from jax.sharding import PartitionSpec as P

HID = 1024
GROUPS = 32
CLASSES = 32
ACTS = 18
TASKS = 64
BLK_DEV = 4
STEPS = 4
WSTART = 16
LANES = 128
PACKED = 40


def normed_rows(values):
    entries = values.shape[-1]
    average = jnp.sum(values, axis=-1, keepdims=True) / entries
    squares = jnp.sum(values * values, axis=-1, keepdims=True) / entries
    return (values - average) * lax.rsqrt(squares - average * average + 1e-05)


def product(rows_in, weight):
    return jnp.dot(rows_in, weight, preferred_element_type=jnp.float32)


def product_nt(rows_in, weight):
    return lax.dot_general(
        rows_in, weight, (((1,), (1,)), ((), ())), preferred_element_type=jnp.float32
    )


def flipped(index, mask):
    bit = 1
    while bit <= mask:
        if mask & bit:
            index = index + bit * (1 - 2 * ((index // bit) % 2))
        bit *= 2
    return index


def window_kernel(
    holders,
    shards,
    groups,
    rows,
    share,
    horizons_ref,
    offsets_ref,
    actions_ref,
    act_ref,
    head_ref,
    deter_ref,
    draws_ref,
    stoch_ref,
    weight_ref,
    prior_ref,
    logit_ref,
    log_prob_ref,
    reward_ref,
    continuation_ref,
    final_ref,
    carried,
    draws,
    act,
    stoch,
    weight,
    prior,
    logit,
    packed,
    spread,
    classes_of,
    embedded,
    horizon,
    own_states,
    own_classes,
    wide,
    hidden,
    gath,
    parts,
    stats,
    leaving,
    passing,
    routed,
    landed,
    found,
    settled,
    fetch_sem,
    send_sem,
    recv_sem,
    stat_send,
    stat_recv,
    pack_send,
    pack_recv,
    leave_send,
    leave_recv,
    route_send,
    route_recv,
    found_send,
    found_recv,
    settled_send,
    settled_recv,
):
    me = lax.axis_index("mp")
    place = lax.axis_index("task")
    peers = {mask: flipped(me, mask) for mask in range(1, shards)}
    rows_here = groups * rows
    block_rows = rows_here // BLK_DEV
    group_blocks = BLK_DEV // groups
    piece = block_rows // holders
    own_rows = rows_here // shards
    padded = own_states.shape[0]
    tasks_here = TASKS // holders
    task_rows = rows_here // tasks_here

    def fetch(k, source_ref, target):
        return pltpu.make_async_copy(source_ref, target, fetch_sem.at[k])

    fetches = [
        fetch(0, draws_ref, draws),
        fetch(1, deter_ref, carried),
        fetch(2, stoch_ref, stoch),
        fetch(3, weight_ref, weight),
        fetch(4, prior_ref, prior),
        fetch(5, logit_ref, logit),
    ]
    for k in range(4):
        fetches[k].start()
    barrier = pltpu.get_barrier_semaphore()

    def ahead_of(ahead):
        return lax.rem(place + ahead, holders)

    for mask in range(1, shards):
        pl.semaphore_signal(
            barrier,
            inc=1,
            device_id={"mp": peers[mask]},
            device_id_type=pl.DeviceIdType.MESH,
        )
    for ahead in range(1, holders):
        pl.semaphore_signal(
            barrier,
            inc=1,
            device_id={"task": ahead_of(ahead)},
            device_id_type=pl.DeviceIdType.MESH,
        )

    def across(source_ref, target_ref, send, recv, ahead):
        return pltpu.make_async_remote_copy(
            src_ref=source_ref,
            dst_ref=target_ref,
            send_sem=send,
            recv_sem=recv,
            device_id={"task": ahead_of(ahead)},
            device_id_type=pl.DeviceIdType.MESH,
        )

    def pack_copy(t, ahead, slot):
        return across(
            packed.at[place, t],
            packed.at[slot, t],
            pack_send.at[t, ahead],
            pack_recv.at[t, ahead],
            ahead,
        )

    def leave_copy(g, ahead):
        return across(
            leaving.at[g, ahead_of(ahead)],
            passing.at[g, place],
            leave_send.at[g, ahead],
            leave_recv.at[g, ahead],
            ahead,
        )

    def route_copy(g, ahead):
        return across(
            routed.at[g, ahead_of(ahead)],
            landed.at[g, place],
            route_send.at[g, ahead],
            route_recv.at[g, ahead],
            ahead,
        )

    def found_copy(ahead):
        return across(
            found.at[place], found.at[place], found_send.at[ahead], found_recv.at[ahead], ahead
        )

    def settled_copy(mask):
        return pltpu.make_async_remote_copy(
            src_ref=settled.at[me],
            dst_ref=settled.at[me],
            send_sem=settled_send.at[mask],
            recv_sem=settled_recv.at[mask],
            device_id={"mp": peers[mask]},
            device_id_type=pl.DeviceIdType.MESH,
        )

    def moved(t, j):
        total = offsets_ref[0, j]
        for s in range(1, STEPS):
            total = total + jnp.where(s <= t, offsets_ref[s, j], 0)
        return lax.rem(total, holders)

    bits = []
    bit = shards // 2
    while bit:
        bits.append(bit)
        bit //= 2
    orders = [bits, [bits[1], bits[0]] + bits[2:]]
    half = rows // 2
    masks = sorted(range(1, shards), key=lambda mask: (mask.bit_count(), mask))

    def source(mask):
        return me if mask == 0 else peers[mask]

    def hop(slot, g, s, mask, via):
        block = gath.at[slot, g, source(mask), pl.ds(s * half, half)]
        return pltpu.make_async_remote_copy(
            src_ref=block,
            dst_ref=block,
            send_sem=send_sem.at[g, s, mask ^ via],
            recv_sem=recv_sem.at[g, s, mask ^ via],
            device_id={"mp": peers[via]},
            device_id_type=pl.DeviceIdType.MESH,
        )

    def forward(slot, g, s, mask):
        order = orders[s]
        last = max([order.index(bit) for bit in order if mask & bit], default=-1)
        for via in order[last + 1 :]:
            hop(slot, g, s, mask, via).start()

    def arriving(slot, g, s, mask):
        block = gath.at[slot, g, source(mask), pl.ds(s * half, half)]
        return pltpu.make_async_remote_copy(
            src_ref=block,
            dst_ref=block,
            send_sem=send_sem.at[g, s, mask],
            recv_sem=recv_sem.at[g, s, mask],
            device_id={"mp": peers[mask]},
            device_id_type=pl.DeviceIdType.MESH,
        )

    def launch(g, slot):
        here = pl.ds(g * rows, rows)
        gath[slot, g, me] = carried[here, :].astype(jnp.bfloat16)
        for s in range(2):
            forward(slot, g, s, 0)

    def stat_copy(g, mask):
        return pltpu.make_async_remote_copy(
            src_ref=stats.at[g, 0],
            dst_ref=stats.at[g, mask],
            send_sem=stat_send.at[g, mask],
            recv_sem=stat_recv.at[g, mask],
            device_id={"mp": peers[mask]},
            device_id_type=pl.DeviceIdType.MESH,
        )

    def multiply(g, rows_in, start, depth, first):
        for part in range(3):
            term = jnp.dot(
                rows_in, weight[part, pl.ds(start, depth), :], preferred_element_type=jnp.float32
            )
            if first:
                parts[g, part] = term
            else:
                parts[g, part] += term

    early = [(s, orders[s][0]) for s in range(2)]

    def relay(slot, g):
        for s, mask in early:
            arriving(slot, g, s, mask).wait_recv()
            forward(slot, g, s, mask)

    def gather_and_multiply(t, slot, g):
        multiply(g, embedded[t, pl.ds(g * rows, rows), :], 0, HID, True)
        for mask in [0] + masks:
            if mask:
                for s in range(2):
                    if (s, mask) not in early:
                        arriving(slot, g, s, mask).wait_recv()
                        forward(slot, g, s, mask)
            start = pl.multiple_of(HID + source(mask) * share, share)
            multiply(g, gath[slot, g, source(mask)], start, share, False)
        sums = jnp.zeros((rows, 128), jnp.float32)
        squares = jnp.zeros((rows, 128), jnp.float32)
        for part in range(3):
            for column in range(0, share, 128):
                piece = parts[g, part, :, pl.ds(column, 128)]
                sums = sums + piece
                squares = squares + piece * piece
        stats[g, 0, 0:1, :] = jnp.sum(sums.T, axis=0, keepdims=True)
        stats[g, 0, 1:2, :] = jnp.sum(squares.T, axis=0, keepdims=True)
        for mask in masks:
            stat_copy(g, mask).start()

    def renew(t, slot, g):
        for mask in masks:
            stat_copy(g, mask).wait()
        total = jnp.sum(stats[g], axis=0) / (3 * share * shards)
        average = jnp.broadcast_to(total[0:1], (128, rows)).T
        square = jnp.broadcast_to(total[1:2], (128, rows)).T
        inverse = lax.rsqrt(square - average * average + 1e-05)
        here = pl.ds(g * rows, rows)
        alive = horizon[here, :] > WSTART + t
        for column in range(0, share, 128):
            where = pl.ds(column, 128)
            normed = [(parts[g, part, :, where] - average) * inverse for part in range(3)]
            reset_gate = jax.nn.sigmoid(normed[0])
            candidate = jnp.tanh(reset_gate * normed[1])
            update = jax.nn.sigmoid(normed[2] - 1.0)
            before = carried[here, where]
            renewed = update * candidate + (1.0 - update) * before
            carried[here, where] = jnp.where(alive, renewed, before)
        for s in range(2):
            for mask in masks:
                arriving(slot, g, s, mask).wait_send()

    def leave(g):
        for b in range(group_blocks):
            for k in range(holders):
                start = g * rows + b * block_rows + k * piece
                leaving[g, k, b] = carried[pl.ds(start, piece), :].astype(jnp.bfloat16)
        for ahead in range(1, holders):
            leave_copy(g, ahead).start()
        passing[g, place] = leaving[g, place]

    def route(g):
        for ahead in range(1, holders):
            leave_copy(g, ahead).wait()
        for d in range(holders):
            for b in range(group_blocks):
                holder = lax.rem(d + holders - moved(STEPS - 1, g * group_blocks + b), holders)
                taken = passing[g, 0, b]
                for h in range(1, holders):
                    taken = jnp.where(holder == h, passing[g, h, b], taken)
                routed[g, d, b] = taken
        for ahead in range(1, holders):
            route_copy(g, ahead).start()
        landed[g, place] = routed[g, place]

    def land(g):
        for ahead in range(1, holders):
            route_copy(g, ahead).wait()
        for b in range(group_blocks):
            for k in range(holders):
                start = g * rows + b * block_rows + k * piece
                final_ref[pl.ds(start, piece), :] = landed[g, k, b].astype(jnp.float32)

    def pack(t):
        top = draws[t].astype(jnp.float32)
        low = jnp.broadcast_to(
            actions_ref[t : t + 1, :].astype(jnp.float32), (PACKED - GROUPS, rows_here)
        )
        packed[place, t] = jnp.concatenate([top, low], axis=0).astype(jnp.bfloat16)
        for ahead in range(1, holders):
            pack_copy(t, ahead, place).start()

    class_row = lax.broadcasted_iota(jnp.int32, (1, GROUPS * CLASSES), 1) % CLASSES
    class_row = class_row.astype(jnp.float32)

    def embed(t):
        for ahead in range(1, holders):
            pack_copy(t, ahead, place).wait()
        block = lax.broadcasted_iota(jnp.int32, (PACKED, rows_here), 1) // block_rows
        holder = jnp.zeros((PACKED, rows_here), jnp.int32)
        for j in range(BLK_DEV):
            holder = jnp.where(block == j, lax.rem(place + moved(t, j), holders), holder)
        home = packed[0, t].astype(jnp.float32)
        for h in range(1, holders):
            home = jnp.where(holder == h, packed[h, t].astype(jnp.float32), home)
        tall = jnp.concatenate([home, jnp.zeros((LANES - PACKED, rows_here), jnp.float32)], axis=0)
        flat = tall.T
        classes_of[t] = flat.astype(jnp.bfloat16)
        for start in range(0, rows_here, LANES):
            here = pl.ds(start, LANES)
            low = classes_of[t, here, :]
            hot = (product(low, spread[...]) == class_row).astype(jnp.bfloat16)
            chosen = low[:, GROUPS : GROUPS + 1].astype(jnp.float32)
            action = lax.broadcasted_iota(jnp.int32, (LANES, LANES), 1).astype(jnp.float32)
            hot_action = (action == chosen).astype(jnp.bfloat16)
            pre = product(hot, stoch[...]) + product(hot_action, act[...])
            embedded[t, here, :] = jax.nn.silu(normed_rows(pre)).astype(jnp.bfloat16)

    def take_own(t, slot):
        first = me * own_rows
        g = first // rows
        within = pl.ds(pl.multiple_of(lax.rem(first, rows), own_rows), own_rows)
        for mask in range(shards):
            start = pl.multiple_of(source(mask) * share, share)
            own_states[pl.ds(pl.multiple_of(t * own_rows, own_rows), own_rows), pl.ds(start, share)] = (
                gath[slot, g, source(mask), within, :]
            )

    def judge():
        wide[...] = product(own_states[...], prior[...])
        hidden[...] = jax.nn.silu(normed_rows(wide[...])).astype(jnp.bfloat16)

    def conclude():
        first = pl.ds(pl.multiple_of(me * own_rows, own_rows), own_rows)
        for t in range(STEPS):
            own_classes[pl.ds(t * own_rows, own_rows), :] = classes_of[t, first, :]
        wide[...] = jnp.exp(5.0 * jnp.tanh(product(hidden[...], logit[...]) / 5.0))
        exponent = wide[...]
        hot = product(own_classes[...], spread[...]) == class_row
        high = exponent.astype(jnp.bfloat16)
        low = (exponent - high.astype(jnp.float32)).astype(jnp.bfloat16)
        none = jnp.zeros_like(high)
        sums = product_nt(high, spread[...]) + product_nt(low, spread[...])
        taken = product_nt(jnp.where(hot, high, none), spread[...]) + product_nt(
            jnp.where(hot, low, none), spread[...]
        )
        lane = lax.broadcasted_iota(jnp.int32, (padded, LANES), 1)
        sums = jnp.where(lane < GROUPS, sums, 1.0)
        chances = jnp.where(lane < GROUPS, 0.99 * taken / sums + 0.01 / CLASSES, 1.0)
        log_prob = jnp.sum(jnp.log(chances), axis=-1, keepdims=True)
        heads = product(hidden[...], head_ref[...])
        living = [
            (horizon[first, :] > WSTART + t).astype(jnp.float32) for t in range(STEPS)
        ]
        if STEPS * own_rows < padded:
            living.append(jnp.zeros((padded - STEPS * own_rows, LANES), jnp.float32))
        living = jnp.concatenate(living, axis=0)
        results = jnp.where(
            lane == 0,
            log_prob,
            jnp.where(lane == 1, heads[:, 0:1], jax.nn.sigmoid(heads[:, 1:2])),
        )
        found[place] = (results * living).T[0:8, :]
        for ahead in range(1, holders):
            found_copy(ahead).start()

    def settle():
        for ahead in range(1, holders):
            found_copy(ahead).wait()
        j = (me * own_rows) // block_rows
        lane = lax.broadcasted_iota(jnp.int32, (8, padded), 1) // own_rows
        mine = jnp.zeros((8, padded), jnp.float32)
        for t in range(STEPS):
            holder = lax.rem(place + holders - moved(t, j), holders)
            mine = jnp.where(lane == t, found[holder], mine)
        settled[me] = mine
        for mask in masks:
            settled_copy(mask).start()

    def publish():
        for mask in masks:
            settled_copy(mask).wait()
        lane = lax.broadcasted_iota(jnp.int32, (8, LANES), 1) // own_rows
        fit = LANES // own_rows
        for start in range(0, rows_here, LANES):
            for t in range(STEPS):
                line = jnp.zeros((8, LANES), jnp.float32)
                for k in range(fit):
                    amount = ((k - t) * own_rows) % LANES
                    whole = settled[start // own_rows + k]
                    if amount:
                        whole = pltpu.roll(whole, amount, 1)
                    line = jnp.where(lane == k, whole, line)
                where = pl.ds(start, LANES)
                log_prob_ref[t : t + 1, where] = line[0:1]
                reward_ref[t : t + 1, where] = line[1:2]
                continuation_ref[t : t + 1, where] = line[2:3]

    for k in range(tasks_here):
        horizon[pl.ds(k * task_rows, task_rows), :] = jnp.full(
            (task_rows, LANES), horizons_ref[place * tasks_here + k], jnp.int32
        )
    group_of = lax.broadcasted_iota(jnp.int32, (LANES, GROUPS * CLASSES), 1) // CLASSES
    spread[...] = (
        group_of == lax.broadcasted_iota(jnp.int32, (LANES, GROUPS * CLASSES), 0)
    ).astype(jnp.bfloat16)
    act[...] = jnp.concatenate(
        [act_ref[...].astype(jnp.float32), jnp.zeros((LANES - ACTS, HID), jnp.float32)], axis=0
    ).astype(jnp.bfloat16)
    if STEPS * own_rows < padded:
        own_states[...] = jnp.zeros_like(own_states)
        own_classes[...] = jnp.zeros_like(own_classes)
    fetches[0].wait()
    fetches[1].wait()
    pl.semaphore_wait(barrier, shards - 1 + holders - 1)
    for g in range(groups):
        launch(g, 0)
    for t in range(STEPS):
        pack(t)
    for g in range(groups):
        relay(0, g)
    fetches[2].wait()

    def embed_step(t, _):
        embed(t)
        return 0

    lax.fori_loop(0, STEPS, embed_step, 0)
    fetches[3].wait()
    fetches[4].start()
    fetches[5].start()

    def step(t, _):
        slot = lax.rem(t, 2)
        going = t < STEPS - 1
        gather_and_multiply(t, slot, 0)
        pl.when(t > 0)(functools.partial(relay, slot, 1))
        renew(t, slot, 0)
        pl.when(going)(functools.partial(launch, 0, 1 - slot))
        pl.when(t == STEPS - 1)(functools.partial(leave, 0))
        gather_and_multiply(t, slot, 1)
        take_own(t, slot)

        @pl.when(going)
        def _():
            relay(1 - slot, 0)
            renew(t, slot, 1)
            launch(1, 1 - slot)

        return 0

    lax.fori_loop(0, STEPS, step, 0)
    fetches[4].wait()
    judge()
    route(0)
    renew(STEPS - 1, (STEPS - 1) % 2, 1)
    leave(1)
    fetches[5].wait()
    conclude()
    route(1)
    land(0)
    settle()
    land(1)
    publish()


def window(deter, draws, actions, horizons, offsets, stoch, act, weight, prior, logit, head):
    holders = lax.axis_size("task")
    shards = lax.axis_size("mp")
    rows_here, share = deter.shape
    groups = 2
    rows = rows_here // groups
    own_rows = rows_here // shards
    padded = max(STEPS * own_rows, LANES)
    piece = rows_here // BLK_DEV // holders
    vmem = pl.BlockSpec(memory_space=pltpu.VMEM)
    smem = pl.BlockSpec(memory_space=pltpu.SMEM)
    hbm = pl.BlockSpec(memory_space=pl.ANY)
    dma = pltpu.SemaphoreType.DMA
    low = jnp.bfloat16
    full = jnp.float32
    line = jax.ShapeDtypeStruct((STEPS, rows_here), full)
    moving = (groups, holders, BLK_DEV // groups, piece, share)
    return pl.pallas_call(
        functools.partial(window_kernel, holders, shards, groups, rows, share),
        out_shape=(line, line, line, jax.ShapeDtypeStruct((rows_here, share), full)),
        in_specs=[smem, smem, vmem, vmem, vmem, hbm, hbm, hbm, hbm, hbm, hbm],
        out_specs=(vmem, vmem, vmem, vmem),
        scratch_shapes=[
            pltpu.VMEM((rows_here, share), full),
            pltpu.VMEM(draws.shape, jnp.int32),
            pltpu.VMEM((LANES, HID), low),
            pltpu.VMEM(stoch.shape, low),
            pltpu.VMEM(weight.shape, low),
            pltpu.VMEM(prior.shape, low),
            pltpu.VMEM(logit.shape, low),
            pltpu.VMEM((holders, STEPS, PACKED, rows_here), low),
            pltpu.VMEM((LANES, GROUPS * CLASSES), low),
            pltpu.VMEM((STEPS, rows_here, LANES), low),
            pltpu.VMEM((STEPS, rows_here, HID), low),
            pltpu.VMEM((rows_here, LANES), jnp.int32),
            pltpu.VMEM((padded, shards * share), low),
            pltpu.VMEM((padded, LANES), low),
            pltpu.VMEM((padded, HID), full),
            pltpu.VMEM((padded, HID), low),
            pltpu.VMEM((2, groups, shards, rows, share), low),
            pltpu.VMEM((groups, 3, rows, share), full),
            pltpu.VMEM((groups, shards, 2, rows), full),
            pltpu.VMEM(moving, low),
            pltpu.VMEM(moving, low),
            pltpu.VMEM(moving, low),
            pltpu.VMEM(moving, low),
            pltpu.VMEM((holders, 8, padded), full),
            pltpu.VMEM((shards, 8, padded), full),
            dma((6,)),
            dma((groups, 2, shards)),
            dma((groups, 2, shards)),
            dma((groups, shards)),
            dma((groups, shards)),
            dma((STEPS, holders)),
            dma((STEPS, holders)),
            dma((groups, holders)),
            dma((groups, holders)),
            dma((groups, holders)),
            dma((groups, holders)),
            dma((holders,)),
            dma((holders,)),
            dma((shards,)),
            dma((shards,)),
        ],
        compiler_params=pltpu.CompilerParams(
            collective_id=0, has_side_effects=True, vmem_limit_bytes=62 * 1024 * 1024
        ),
    )(horizons, offsets, actions, act, head, deter, draws, stoch, weight, prior, logit)


def on_device(
    deter,
    draws,
    actions,
    horizons,
    offsets,
    embed_stoch,
    embed_act,
    gru_weight,
    prior_weight,
    logit_weight,
    head_weight,
):
    return window(
        deter,
        draws,
        actions,
        horizons,
        offsets,
        embed_stoch,
        embed_act,
        jnp.transpose(gru_weight, (1, 0, 2)),
        prior_weight,
        logit_weight,
        head_weight,
    )


def solution(mesh):
    in_specs = (
        P("task", "mp"),
        P(None, None, "task"),
        P(None, "task"),
        P(),
        P(),
        P(),
        P(),
        P(None, None, "mp"),
        P(),
        P(),
        P(),
    )
    out_specs = (P(None, "task"), P(None, "task"), P(None, "task"), P("task", "mp"))
    return jax.shard_map(
        on_device, mesh=mesh, in_specs=in_specs, out_specs=out_specs, check_vma=False
    )
```

time: 144 us -> 100 us (0.69)
  Pallas kernels: 104 us -> 91.9 us
  matrix products: 11.3 us -> 0 us
  other arithmetic: 10.1 us -> 0 us
  starting transfers between devices: 5.44 us -> 0 us
  local copies, waits for them, and re-layouts: 11.2 us -> 7.24 us
    pallas_call x4 -> x1, Pallas kernels: 104 us -> 91.9 us  [window(): pl.pallas_call(functools.partial(window_kernel, holders, shards, groups,...]
    dot_general x5 -> x0, matrix products: 11.3 us -> none  [product(): return jnp.dot(rows_in, weight, preferred_element_type=jnp.float32)]
    unnamed x14 -> x5, local copies, waits for them, and re-layouts: 1.44 us -> 7.24 us
    all_to_all x1 -> x0, starting transfers between devices: 5.44 us -> none  [on_device(): lax.all_to_all(outgoing.reshape(holders * BLK_DEV * block_rows, det_share...]
    reduce_sum x6 -> x0, other arithmetic: 3.6 us -> none  [the longest x1 1.25 us: on_device(): chosen = jnp.sum(jnp.where(own_hot, exponent, 0.0), axis=-1)]
    convert_element_type x5 -> x0, other arithmetic: 3.22 us -> none  [the longest x1 1.6 us: on_device(): embedded = jax.nn.silu(normed_rows(embed_pre)).astype(jnp.bfloat16)]
    exp x1 -> x0, local copies, waits for them, and re-layouts: 2.03 us -> none  [on_device(): exponent = jnp.exp(5.0 * jnp.tanh(raw / 5.0))]
    squeeze x3 -> x0, local copies, waits for them, and re-layouts: 2.01 us -> none  [on_device(): return (outs[0], outs[1], outs[2], final)]
  transfers between devices with their start and end apart: 1 -> 0, of which waited for: 0 -> 0; matrix products, arithmetic and copies ran while one was open for 13% -> 0% of each run, Pallas kernels for 11% -> 0%
where the time goes in v1:
time: 100 us; the launch traced here: 99.8 us
  Pallas kernels  91.9 us (92%)
  local copies, waits for them, and re-layouts  7.24 us (7%)
    pallas_call x1, Pallas kernels, window(): pl.pallas_call(functools.partial(window_kernel, holders, shards, groups,...  91.9 us
    unnamed x5, local copies, waits for them, and re-layouts  7.24 us

profile of v1, /device:TPU:0, one launch (start us, length us, event | category | flops | bytes accessed | tf_op | source)
XLA Modules:
  0.0 99.8 jit_solution(1914827564170381504)
XLA Ops:
  0.6 1.6 %copy.15.head_ref = bf16[1024,2]{1,0:T(8,128)(2,1)} copy(bf16[1024,2]{0,1:T(2,128)(2,1)} %param.21) | data formatting | bytes 8192 | tf_op args[10]
  2.2 91.9 %shard_map.138 = (f32[4,256]{1,0:T(4,128)}, f32[4,256]{1,0:T(4,128)}, f32[4,256]{1,0:T(4,128)}, f32[256,512]{1,0:T(8,128)}) custom-call(s32[64]{0:T(128)} %horizons_ref.1, s32[4,4]{1,0:T(4,128)} %offsets_ref.1, s32[4,256]{1,0:T(4,128)} %actions_ref.1, bf16[18,1024]{1,0:T(8,128)(2,1)} %act_ref.1, bf16[1024,2]{1,0:T(8,128)(2,1)} %copy.15.head_ref, ...), custom_call_target="tpu_custom_call" | custom-call | tf_op jit(solution)/shard_map/pallas_call | solution.py:561
  94.2 1.3 %copy.20 = f32[4,256]{1,0:T(4,128)} copy(f32[4,256]{1,0:T(4,128)} %get-tuple-element.8) | data formatting | bytes 8192
  95.4 1.3 %copy.21 = f32[4,256]{1,0:T(4,128)} copy(f32[4,256]{1,0:T(4,128)} %get-tuple-element.9) | data formatting | bytes 8192
  96.7 1.3 %copy.22 = f32[4,256]{1,0:T(4,128)} copy(f32[4,256]{1,0:T(4,128)} %get-tuple-element.10) | data formatting | bytes 8192
  98.0 1.9 %copy.23 = f32[256,512]{1,0:T(8,128)} copy(f32[256,512]{1,0:T(8,128)} %get-tuple-element.11) | data formatting | bytes 1048576

commit v2 on v1

--- a/solution.py
+++ b/solution.py
@@ -17,6 +17,7 @@
 WSTART = 16
 LANES = 128
 PACKED = 40
+CUTS = 4
 
 
 def normed_rows(values):
@@ -62,10 +63,8 @@
     weight_ref,
     prior_ref,
     logit_ref,
-    log_prob_ref,
-    reward_ref,
-    continuation_ref,
-    final_ref,
+    lines_ref,
+    landed,
     carried,
     draws,
     act,
@@ -88,7 +87,6 @@
     leaving,
     passing,
     routed,
-    landed,
     found,
     settled,
     fetch_sem,
@@ -171,21 +169,21 @@
             ahead,
         )
 
-    def leave_copy(g, ahead):
+    def leave_copy(j, ahead):
         return across(
-            leaving.at[g, ahead_of(ahead)],
-            passing.at[g, place],
-            leave_send.at[g, ahead],
-            leave_recv.at[g, ahead],
+            leaving.at[j, ahead_of(ahead)],
+            passing.at[j, place],
+            leave_send.at[j, ahead],
+            leave_recv.at[j, ahead],
             ahead,
         )
 
-    def route_copy(g, ahead):
+    def route_copy(j, ahead):
         return across(
-            routed.at[g, ahead_of(ahead)],
-            landed.at[g, place],
-            route_send.at[g, ahead],
-            route_recv.at[g, ahead],
+            routed.at[j, ahead_of(ahead)],
+            landed.at[j, place],
+            route_send.at[j, ahead],
+            route_recv.at[j, ahead],
             ahead,
         )
 
@@ -216,14 +214,14 @@
         bits.append(bit)
         bit //= 2
     orders = [bits, [bits[1], bits[0]] + bits[2:]]
-    half = rows // 2
+    size = rows // CUTS
     masks = sorted(range(1, shards), key=lambda mask: (mask.bit_count(), mask))
 
     def source(mask):
         return me if mask == 0 else peers[mask]
 
     def hop(slot, g, s, mask, via):
-        block = gath.at[slot, g, source(mask), pl.ds(s * half, half)]
+        block = gath.at[slot, g, source(mask), pl.ds(s * size, size)]
         return pltpu.make_async_remote_copy(
             src_ref=block,
             dst_ref=block,
@@ -234,13 +232,13 @@
         )
 
     def forward(slot, g, s, mask):
-        order = orders[s]
+        order = orders[s % 2]
         last = max([order.index(bit) for bit in order if mask & bit], default=-1)
         for via in order[last + 1 :]:
             hop(slot, g, s, mask, via).start()
 
     def arriving(slot, g, s, mask):
-        block = gath.at[slot, g, source(mask), pl.ds(s * half, half)]
+        block = gath.at[slot, g, source(mask), pl.ds(s * size, size)]
         return pltpu.make_async_remote_copy(
             src_ref=block,
             dst_ref=block,
@@ -253,7 +251,7 @@
     def launch(g, slot):
         here = pl.ds(g * rows, rows)
         gath[slot, g, me] = carried[here, :].astype(jnp.bfloat16)
-        for s in range(2):
+        for s in range(CUTS):
             forward(slot, g, s, 0)
 
     def stat_copy(g, mask):
@@ -276,7 +274,10 @@
             else:
                 parts[g, part] += term
 
-    early = [(s, orders[s][0]) for s in range(2)]
+    early = [(s, orders[s % 2][0]) for s in range(CUTS)]
+
+    near = [mask for mask in masks if mask % 2 == 0 and mask.bit_count() == 1]
+    far = [mask for mask in masks if mask % 2 == 0 and mask.bit_count() > 1]
 
     def relay(slot, g):
         for s, mask in early:
@@ -284,15 +285,35 @@
             forward(slot, g, s, mask)
 
     def gather_and_multiply(t, slot, g):
-        multiply(g, embedded[t, pl.ds(g * rows, rows), :], 0, HID, True)
-        for mask in [0] + masks:
-            if mask:
-                for s in range(2):
-                    if (s, mask) not in early:
-                        arriving(slot, g, s, mask).wait_recv()
-                        forward(slot, g, s, mask)
+        def arrive(mask):
+            for s in range(CUTS):
+                if (s, mask) not in early:
+                    arriving(slot, g, s, mask).wait_recv()
+                    forward(slot, g, s, mask)
+
+        def take(mask):
             start = pl.multiple_of(HID + source(mask) * share, share)
             multiply(g, gath[slot, g, source(mask)], start, share, False)
+
+        for mask in near:
+            arrive(mask)
+        multiply(g, embedded[t, pl.ds(g * rows, rows), :], 0, HID, True)
+        take(0)
+        arrive(1)
+        take(1)
+        for mask in near[:-1]:
+            take(mask)
+        for mask in far:
+            arrive(mask)
+        take(near[-1])
+        rest = [mask for mask in masks if mask % 2 and mask > 1]
+        for mask in rest[:-1]:
+            arrive(mask)
+            take(mask)
+        for mask in far:
+            take(mask)
+        arrive(rest[-1])
+        take(rest[-1])
         sums = jnp.zeros((rows, 128), jnp.float32)
         squares = jnp.zeros((rows, 128), jnp.float32)
         for part in range(3):
@@ -323,40 +344,38 @@
             before = carried[here, where]
             renewed = update * candidate + (1.0 - update) * before
             carried[here, where] = jnp.where(alive, renewed, before)
-        for s in range(2):
+        for s in range(CUTS):
             for mask in masks:
                 arriving(slot, g, s, mask).wait_send()
 
-    def leave(g):
-        for b in range(group_blocks):
-            for k in range(holders):
-                start = g * rows + b * block_rows + k * piece
-                leaving[g, k, b] = carried[pl.ds(start, piece), :].astype(jnp.bfloat16)
+    def leave(j):
+        for k in range(holders):
+            start = j * block_rows + k * piece
+            leaving[j, k] = carried[pl.ds(start, piece), :].astype(jnp.bfloat16)
         for ahead in range(1, holders):
-            leave_copy(g, ahead).start()
-        passing[g, place] = leaving[g, place]
-
-    def route(g):
+            leave_copy(j, ahead).start()
+        passing[j, place] = leaving[j, place]
+
+    def leave_group(g):
+        for j in range(g * group_blocks, (g + 1) * group_blocks):
+            leave(j)
+
+    def route(j):
         for ahead in range(1, holders):
-            leave_copy(g, ahead).wait()
+            leave_copy(j, ahead).wait()
         for d in range(holders):
-            for b in range(group_blocks):
-                holder = lax.rem(d + holders - moved(STEPS - 1, g * group_blocks + b), holders)
-                taken = passing[g, 0, b]
-                for h in range(1, holders):
-                    taken = jnp.where(holder == h, passing[g, h, b], taken)
-                routed[g, d, b] = taken
+            holder = lax.rem(d + holders - moved(STEPS - 1, j), holders)
+            taken = passing[j, 0]
+            for h in range(1, holders):
+                taken = jnp.where(holder == h, passing[j, h], taken)
+            routed[j, d] = taken
         for ahead in range(1, holders):
-            route_copy(g, ahead).start()
-        landed[g, place] = routed[g, place]
-
-    def land(g):
+            route_copy(j, ahead).start()
+        landed[j, place] = routed[j, place]
+
+    def land(j):
         for ahead in range(1, holders):
-            route_copy(g, ahead).wait()
-        for b in range(group_blocks):
-            for k in range(holders):
-                start = g * rows + b * block_rows + k * piece
-                final_ref[pl.ds(start, piece), :] = landed[g, k, b].astype(jnp.float32)
+            route_copy(j, ahead).wait()
 
     def pack(t):
         top = draws[t].astype(jnp.float32)
@@ -425,7 +444,7 @@
         sums = jnp.where(lane < GROUPS, sums, 1.0)
         chances = jnp.where(lane < GROUPS, 0.99 * taken / sums + 0.01 / CLASSES, 1.0)
         log_prob = jnp.sum(jnp.log(chances), axis=-1, keepdims=True)
-        heads = product(hidden[...], head_ref[...])
+        heads = product_nt(hidden[...], head_ref[...])
         living = [
             (horizon[first, :] > WSTART + t).astype(jnp.float32) for t in range(STEPS)
         ]
@@ -469,9 +488,7 @@
                         whole = pltpu.roll(whole, amount, 1)
                     line = jnp.where(lane == k, whole, line)
                 where = pl.ds(start, LANES)
-                log_prob_ref[t : t + 1, where] = line[0:1]
-                reward_ref[t : t + 1, where] = line[1:2]
-                continuation_ref[t : t + 1, where] = line[2:3]
+                lines_ref[t, :, where] = line
 
     for k in range(tasks_here):
         horizon[pl.ds(k * task_rows, task_rows), :] = jnp.full(
@@ -498,11 +515,7 @@
         relay(0, g)
     fetches[2].wait()
 
-    def embed_step(t, _):
-        embed(t)
-        return 0
-
-    lax.fori_loop(0, STEPS, embed_step, 0)
+    embed(0)
     fetches[3].wait()
     fetches[4].start()
     fetches[5].start()
@@ -512,9 +525,12 @@
         going = t < STEPS - 1
         gather_and_multiply(t, slot, 0)
         pl.when(t > 0)(functools.partial(relay, slot, 1))
+        pl.when(t == 0)(functools.partial(embed, 1))
+        pl.when(t == 1)(functools.partial(embed, 2))
+        pl.when(t == 2)(functools.partial(embed, 3))
         renew(t, slot, 0)
         pl.when(going)(functools.partial(launch, 0, 1 - slot))
-        pl.when(t == STEPS - 1)(functools.partial(leave, 0))
+        pl.when(t == STEPS - 1)(functools.partial(leave_group, 0))
         gather_and_multiply(t, slot, 1)
         take_own(t, slot)
 
@@ -529,16 +545,43 @@
     lax.fori_loop(0, STEPS, step, 0)
     fetches[4].wait()
     judge()
-    route(0)
+    for j in range(group_blocks):
+        route(j)
     renew(STEPS - 1, (STEPS - 1) % 2, 1)
-    leave(1)
+    leave_group(1)
     fetches[5].wait()
     conclude()
-    route(1)
-    land(0)
+    for j in range(group_blocks, BLK_DEV):
+        route(j)
     settle()
-    land(1)
     publish()
+    for j in range(BLK_DEV):
+        land(j)
+
+
+def hand_out_kernel(lines_ref, landed_ref, log_prob_ref, reward_ref, continuation_ref, final_ref):
+    blocks, holders, piece, share = landed_ref.shape
+    for k, target in enumerate((log_prob_ref, reward_ref, continuation_ref)):
+        for t in range(STEPS):
+            target[t : t + 1, :] = lines_ref[t, k : k + 1, :]
+    for j in range(blocks):
+        for k in range(holders):
+            start = (j * holders + k) * piece
+            final_ref[pl.ds(start, piece), :] = landed_ref[j, k].astype(jnp.float32)
+
+
+def hand_out(lines, landed):
+    blocks, holders, piece, share = landed.shape
+    rows_here = blocks * holders * piece
+    line = jax.ShapeDtypeStruct((STEPS, rows_here), jnp.float32)
+    vmem = pl.BlockSpec(memory_space=pltpu.VMEM)
+    return pl.pallas_call(
+        hand_out_kernel,
+        out_shape=(line, line, line, jax.ShapeDtypeStruct((rows_here, share), jnp.float32)),
+        in_specs=[vmem, vmem],
+        out_specs=(vmem, vmem, vmem, vmem),
+        compiler_params=pltpu.CompilerParams(vmem_limit_bytes=4 * 1024 * 1024),
+    )(lines, landed)
 
 
 def window(deter, draws, actions, horizons, offsets, stoch, act, weight, prior, logit, head):
@@ -556,13 +599,15 @@
     dma = pltpu.SemaphoreType.DMA
     low = jnp.bfloat16
     full = jnp.float32
-    line = jax.ShapeDtypeStruct((STEPS, rows_here), full)
-    moving = (groups, holders, BLK_DEV // groups, piece, share)
+    moving = (BLK_DEV, holders, piece, share)
     return pl.pallas_call(
         functools.partial(window_kernel, holders, shards, groups, rows, share),
-        out_shape=(line, line, line, jax.ShapeDtypeStruct((rows_here, share), full)),
+        out_shape=(
+            jax.ShapeDtypeStruct((STEPS, 8, rows_here), full),
+            jax.ShapeDtypeStruct(moving, low),
+        ),
         in_specs=[smem, smem, vmem, vmem, vmem, hbm, hbm, hbm, hbm, hbm, hbm],
-        out_specs=(vmem, vmem, vmem, vmem),
+        out_specs=(vmem, vmem),
         scratch_shapes=[
             pltpu.VMEM((rows_here, share), full),
             pltpu.VMEM(draws.shape, jnp.int32),
@@ -586,20 +631,19 @@
             pltpu.VMEM(moving, low),
             pltpu.VMEM(moving, low),
             pltpu.VMEM(moving, low),
-            pltpu.VMEM(moving, low),
             pltpu.VMEM((holders, 8, padded), full),
             pltpu.VMEM((shards, 8, padded), full),
             dma((6,)),
-            dma((groups, 2, shards)),
-            dma((groups, 2, shards)),
+            dma((groups, CUTS, shards)),
+            dma((groups, CUTS, shards)),
             dma((groups, shards)),
             dma((groups, shards)),
             dma((STEPS, holders)),
             dma((STEPS, holders)),
-            dma((groups, holders)),
-            dma((groups, holders)),
-            dma((groups, holders)),
-            dma((groups, holders)),
+            dma((BLK_DEV, holders)),
+            dma((BLK_DEV, holders)),
+            dma((BLK_DEV, holders)),
+            dma((BLK_DEV, holders)),
             dma((holders,)),
             dma((holders,)),
             dma((shards,)),
@@ -624,7 +668,7 @@
     logit_weight,
     head_weight,
 ):
-    return window(
+    lines, landed = window(
         deter,
         draws,
         actions,
@@ -635,8 +679,9 @@
         jnp.transpose(gru_weight, (1, 0, 2)),
         prior_weight,
         logit_weight,
-        head_weight,
+        jnp.transpose(head_weight),
     )
+    return hand_out(lines, landed)
 
 
 def solution(mesh):

time: 100 us -> 82.8 us (0.83)
  Pallas kernels: 91.9 us -> 80.2 us
  local copies, waits for them, and re-layouts: 7.24 us -> 1.7 us
    pallas_call x1, Pallas kernels: 91.9 us -> 79.3 us  [window(): pl.pallas_call(functools.partial(window_kernel, holders, shards, groups,...]
    unnamed x5 -> x4, local copies, waits for them, and re-layouts: 7.24 us -> 1.7 us
where the time goes in v2:
time: 82.8 us; the launch traced here: 82.5 us
  Pallas kernels  80.2 us (97%)
  local copies, waits for them, and re-layouts  1.7 us (2%)
    pallas_call x1, Pallas kernels, window(): pl.pallas_call(functools.partial(window_kernel, holders, shards, groups,...  79.3 us
    unnamed x4, local copies, waits for them, and re-layouts  1.7 us

profile of v2, /device:TPU:0, one launch (start us, length us, event | category | flops | bytes accessed | tf_op | source)
XLA Modules:
  0.0 82.5 jit_solution(9090352805969665879)
XLA Ops:
  0.6 79.3 %shard_map.138 = (f32[4,8,256]{2,1,0:T(8,128)}, bf16[4,4,16,512]{3,2,1,0:T(8,128)(2,1)}) custom-call(s32[64]{0:T(128)} %horizons_ref.1, s32[4,4]{1,0:T(4,128)} %offsets_ref.1, s32[4,256]{1,0:T(4,128)} %actions_ref.1, bf16[18,1024]{1,0:T(8,128)(2,1)} %act_ref.1, bf16[2,1024]{1,0:T(2,128)(2,1)} %bitcast.3, f32[256,512]{1,0:T(8,128)} %deter_ref.1, ...), custom_call_target="tpu_custom_call" | custom-call | tf_op jit(solution)/shard_map/pallas_call | solution.py:603
  80.0 0.0 copy-start
  80.0 0.9 %copy-done = bf16[4,4,16,512]{3,2,1,0:T(8,128)(2,1)S(1)} copy-done((bf16[4,4,16,512]{3,2,1,0:T(8,128)(2,1)S(1)}, bf16[4,4,16,512]{3,2,1,0:T(8,128)(2,1)}, u32[]{:S(2)}) %copy-start) | copy-done | bytes 262168
  80.9 0.0 copy-start.1
  80.9 0.8 copy-done.1
  81.7 0.8 %shard_map.139 = (f32[4,256]{1,0:T(4,128)}, f32[4,256]{1,0:T(4,128)}, f32[4,256]{1,0:T(4,128)}, f32[256,512]{1,0:T(8,128)}) custom-call(f32[4,8,256]{2,1,0:T(8,128)S(1)} %copy-done.1, bf16[4,4,16,512]{3,2,1,0:T(8,128)(2,1)S(1)} %copy-done), custom_call_target="tpu_custom_call" | custom-call | tf_op jit(solution)/shard_map/pallas_call | solution.py:578
Async XLA Ops:
  80.0 1.0 %copy-start = (bf16[4,4,16,512]{3,2,1,0:T(8,128)(2,1)S(1)}, bf16[4,4,16,512]{3,2,1,0:T(8,128)(2,1)}, u32[]{:S(2)}) copy-start(bf16[4,4,16,512]{3,2,1,0:T(8,128)(2,1)} %get-tuple-element.7.landed_ref) | copy-start | bytes 786436
  80.9 0.8 copy-start.1
